TPU v7x, 32 devices: a whole 2x2x4 slice. The times are simulated.
32 devices in a mesh: samp: 8 (over y, x, core), cpg: 4 (over z).
Axes of the slice: x: 2, y: 2, z: 4, core: 2. Of those that a mesh axis runs over, the one named last changes fastest.
Arguments:
- responses: bfloat16 [256, 16384], P('samp', 'cpg'), may hold values from -5 to 5
- weights: bfloat16 [256, 16384], P('samp', 'cpg'), may hold values from 1 to 8
- phenotype: float32 [16384], P('cpg'), may hold values from -6 to 6
- eigvecs: bfloat16 [16384, 16384], P('cpg', 'samp'), may hold values from -0.046875 to 0.046875
- eigvals: float32 [16384], P('samp'), may hold values from 0.0001 to 1
- positions: int32 [256], replicated, may hold values from 1 to 76800, as said below
- reaches: int32 [256], P('cpg'), may hold values from 1 to 8
Outputs:
- smoothed: float32 [256], P('cpg')
- log_scale: float32 [256], P('cpg')
Inputs may be any that keep to these rules, and one draw needn't show every extreme that they name: CpG m (from 0) lies at 300 m plus an offset of 1 to 300, so positions strictly increase and consecutive CpGs lie 1 to 599 base pairs apart.
All inputs are finite; a program needn't handle non-finite values.
Results may differ from a plain program's by a relative error of at most 0.0041.
Values may be sent and summed in bfloat16 or wider, within the bound.
A program may use at most 64 MiB of HBM per device.

v0:
```python
import jax
import jax.numpy as jnp
from jax import lax
from jax.sharding import PartitionSpec as P

ITERS = 4
HALO = 8


EPSILON = 1e-06
band_width = 1000.0


def padded(value, sides, width):
    for axis, dim in sides:
        peers, length = (lax.axis_size(axis), value.shape[dim])
        up = [(i, (i + 1) % peers) for i in range(peers - 1)]
        down = [(j, i) for i, j in up]
        last = lax.slice_in_dim(value, length - width, length, axis=dim)
        leading = lax.slice_in_dim(value, 0, width, axis=dim)
        before = lax.ppermute(last, axis, up)
        after = lax.ppermute(leading, axis, down)
        value = jnp.concatenate([before, value, after], axis=dim)
    return value


def smooth_block(widened, places, present, reaches):
    block_len = reaches.shape[0]
    centre = places[HALO : HALO + block_len]
    total_sum = jnp.zeros((block_len,), jnp.float32)
    norm_sum = jnp.zeros((block_len,), jnp.float32)
    for offset in range(2 * HALO + 1):
        near_scores = widened[offset : offset + block_len]
        near_places = places[offset : offset + block_len]
        within = (abs(offset - HALO) <= reaches).astype(jnp.float32)
        kernel = (
            present[offset : offset + block_len]
            * within
            * jnp.exp(-jnp.abs(near_places - centre) / band_width)
        )
        total_sum = total_sum + kernel * near_scores
        norm_sum = norm_sum + kernel
    return total_sum / norm_sum


def fit_scores(rot_resp, rot_design, eigen_part, sum_axis, fit_total, score_total):
    log_scale = jnp.zeros((rot_resp.shape[1 - sum_axis],), jnp.float32)
    for repeat in range(ITERS):
        inverse = 1.0 / (jnp.expand_dims(jnp.exp(log_scale), sum_axis) * eigen_part + 1.0)
        design_over = rot_design * inverse
        crossed_part = jnp.sum(design_over * rot_resp, axis=sum_axis)
        energy_part = jnp.sum(design_over * rot_design, axis=sum_axis)
        leverage = eigen_part * inverse
        traced_part = jnp.sum(leverage + 0.0 * inverse, axis=sum_axis)
        fisher_part = jnp.sum(leverage * leverage, axis=sum_axis)
        scaled = leverage * inverse
        resp_part = jnp.sum(scaled * rot_resp * rot_resp, axis=sum_axis)
        mixed_part = jnp.sum(scaled * rot_design * rot_resp, axis=sum_axis)
        design_part = jnp.sum(scaled * rot_design * rot_design, axis=sum_axis)
        crossed, energy, traced, fisher, resp_spread, mixed_spread, design_spread = fit_total(
            (
                crossed_part,
                energy_part,
                traced_part,
                fisher_part,
                resp_part,
                mixed_part,
                design_part,
            )
        )
        energy = energy + EPSILON
        effect = crossed / energy
        spread = resp_spread - 2.0 * effect * mixed_spread + effect * effect * design_spread
        gradient = 0.5 * (spread - traced)
        log_scale = log_scale + jnp.tanh(gradient / (jnp.exp(log_scale) * (0.5 * fisher)))
    inverse = 1.0 / (jnp.expand_dims(jnp.exp(log_scale), sum_axis) * eigen_part + 1.0)
    design_over = rot_design * inverse
    crossed, energy = score_total(
        (
            jnp.sum(design_over * rot_resp, axis=sum_axis),
            jnp.sum(design_over * rot_design, axis=sum_axis),
        )
    )
    return (crossed / jnp.sqrt(energy + EPSILON), log_scale)


def shards(responses, weights, phenotype, eigvecs, eigvals, positions, reaches):
    root_weight = jnp.sqrt(weights.astype(jnp.float32))
    weighted = (root_weight * responses.astype(jnp.float32)).astype(jnp.bfloat16)
    design = (root_weight * phenotype[None, :]).astype(jnp.bfloat16)
    all_resp, all_design = (
        lax.all_gather(weighted, "samp", axis=0, tiled=True),
        lax.all_gather(design, "samp", axis=0, tiled=True),
    )
    cpg_count = lax.axis_size("cpg")
    block_len = reaches.shape[0]
    total_cpgs = block_len * cpg_count
    base = lax.axis_index("cpg") * block_len

    def fit_block(partials):
        return lax.psum(partials, "samp")

    def score_block(partials):
        return lax.psum(partials, "samp")

    rotated = lax.psum_scatter(
        jnp.concatenate(
            [
                jnp.dot(all_resp, eigvecs, preferred_element_type=jnp.float32),
                jnp.dot(all_design, eigvecs, preferred_element_type=jnp.float32),
            ],
            axis=1,
        ),
        "cpg",
        scatter_dimension=0,
        tiled=True,
    )
    comp_width = eigvecs.shape[1]
    scores, log_scale = fit_scores(
        rotated[:, :comp_width],
        rotated[:, comp_width:],
        eigvals[None, :],
        1,
        fit_block,
        score_block,
    )
    widened = padded(scores, (("cpg", 0),), HALO)
    places = lax.dynamic_slice_in_dim(
        jnp.pad(positions.astype(jnp.float32), HALO), base, block_len + 2 * HALO, 0
    )
    global_index = base - HALO + jnp.arange(block_len + 2 * HALO, dtype=jnp.int32)
    present = ((global_index >= 0) & (global_index < total_cpgs)).astype(jnp.float32)
    smoothed = smooth_block(widened, places, present, reaches)
    return (smoothed, log_scale)


def solution(mesh):
    in_specs = (
        P("samp", "cpg"),
        P("samp", "cpg"),
        P("cpg"),
        P("cpg", "samp"),
        P("samp"),
        P(),
        P("cpg"),
    )
    out_specs = (P("cpg"), P("cpg"))
    return jax.shard_map(shards, mesh=mesh, in_specs=in_specs, out_specs=out_specs, check_vma=False)
```

profile of v0, /device:TPU:0, one launch (start us, length us, event | category | flops | bytes accessed | tf_op | source)
XLA Modules:
  0.0 242.1 jit_solution(15517261634825529933)
XLA Ops:
  7.2 2.0 multiply_convert_fusion.1
  9.3 0.7 all-gather.5.cloned.1.call-update
  10.1 30.3 %all-gather.3.cloned.1.call-done = bf16[256,4096]{1,0:T(8,128)(2,1)} async-done(((bf16[32,4096]{1,0:T(8,128)(2,1)}), bf16[256,4096]{1,0:T(8,128)(2,1)}) %all-gather.3.cloned.1.call-update) | async-done | bytes 2097168 | tf_op jit(solution)/shard_map/all_gather | solution.py:92
  40.4 8.7 %fusion.38 = f32[256,2048]{1,0:T(8,128)S(1)} fusion(bf16[256,4096]{1,0:T(8,128)(2,1)} %all-gather.3.cloned.1.call-done, bf16[4096,2048]{1,0:T(8,128)(2,1)} %param.10), kind=kOutput, calls=%fused_computation.110 | convolution fusion | flops 4294967296 | bytes 20971520 | tf_op jit(solution)/shard_map/dot_general | solution.py:109
  49.1 21.0 %all-gather.5.cloned.1.call-done = bf16[256,4096]{1,0:T(8,128)(2,1)} async-done(((bf16[32,4096]{1,0:T(8,128)(2,1)}), bf16[256,4096]{1,0:T(8,128)(2,1)}) %all-gather.5.cloned.1.call-update) | async-done | bytes 2097168 | tf_op jit(solution)/shard_map/all_gather | solution.py:93
  70.1 8.7 %fusion.39 = f32[256,2048]{1,0:T(8,128)S(1)} fusion(bf16[256,4096]{1,0:T(8,128)(2,1)} %all-gather.5.cloned.1.call-done, bf16[4096,2048]{1,0:T(8,128)(2,1)} %param.10), kind=kOutput, calls=%fused_computation.111 | convolution fusion | flops 4294967296 | bytes 20971520 | tf_op jit(solution)/shard_map/dot_general | solution.py:110
  78.8 2.3 pad_maximum_fusion
  81.2 0.6 copy-done.2
  81.9 0.6 multiply_multiply_fusion.14
  82.5 75.6 %reduce-scatter.2.cloned.1.call-done = f32[64,4096]{1,0:T(8,128)} async-done(((f32[256,4096]{1,0:T(8,128)}), f32[64,4096]{1,0:T(8,128)}) %reduce-scatter.2.cloned.1.call-update) | async-done | bytes 1048592 | tf_op jit(solution)/shard_map/reduce_scatter | solution.py:106
  158.1 1.7 fusion.7
  159.8 0.7 reduce_sum.280
  160.5 0.6 reduce_sum.282
  161.1 13.3 %all-reduce.5 = (f32[64]{0:T(128)S(1)}, f32[64]{0:T(128)S(1)}, f32[64]{0:T(128)S(1)}, f32[64]{0:T(128)S(1)}, f32[64]{0:T(128)S(1)}, /*index=5*/f32[64]{0:T(128)S(1)}, f32[64]{0:T(128)S(1)}) all-reduce(f32[64]{0:T(128)S(1)} %reduce_sum.282, f32[64]{0:T(128)S(1)} %reduce_sum.280, ...), channel_id=1, replica_groups=mesh['samp'=8,'cpg'=4] {'samp'}, use_global_device_ids=true, to_apply=%region_14.0 | all-reduce | flops 448 | bytes 3584 | tf_op jit(solution)/shard_map/psum | solution.py:101
  174.4 1.9 multiply_reduce_fusion.12
  176.3 11.8 %all-reduce.4 = (f32[64]{0:T(128)S(1)}, f32[64]{0:T(128)S(1)}, f32[64]{0:T(128)S(1)}, f32[64]{0:T(128)S(1)}, f32[64]{0:T(128)S(1)}, /*index=5*/f32[64]{0:T(128)S(1)}, f32[64]{0:T(128)S(1)}) all-reduce(f32[64]{0:T(128)S(1)} %get-tuple-element.31, f32[64]{0:T(128)S(1)} %get-tuple-element.32, ...), channel_id=1, replica_groups=mesh['samp'=8,'cpg'=4] {'samp'}, use_global_device_ids=true, to_apply=%region_28.0 | all-reduce | flops 448 | bytes 3584 | tf_op jit(solution)/shard_map/psum | solution.py:101
  188.8 11.8 %all-reduce.3 = (f32[64]{0:T(128)S(1)}, f32[64]{0:T(128)S(1)}, f32[64]{0:T(128)S(1)}, f32[64]{0:T(128)S(1)}, f32[64]{0:T(128)S(1)}, /*index=5*/f32[64]{0:T(128)S(1)}, f32[64]{0:T(128)S(1)}) all-reduce(f32[64]{0:T(128)S(1)} %get-tuple-element.29, f32[64]{0:T(128)S(1)} %get-tuple-element.30, ...), channel_id=1, replica_groups=mesh['samp'=8,'cpg'=4] {'samp'}, use_global_device_ids=true, to_apply=%region_42.0 | all-reduce | flops 448 | bytes 3584 | tf_op jit(solution)/shard_map/psum | solution.py:101
  200.6 0.6 multiply_reduce_fusion.4
  201.2 11.8 %all-reduce.2 = (f32[64]{0:T(128)S(1)}, f32[64]{0:T(128)S(1)}, f32[64]{0:T(128)S(1)}, f32[64]{0:T(128)S(1)}, f32[64]{0:T(128)S(1)}, /*index=5*/f32[64]{0:T(128)S(1)}, f32[64]{0:T(128)S(1)}) all-reduce(f32[64]{0:T(128)S(1)} %get-tuple-element.27, f32[64]{0:T(128)S(1)} %get-tuple-element.28, ...), channel_id=1, replica_groups=mesh['samp'=8,'cpg'=4] {'samp'}, use_global_device_ids=true, to_apply=%region_56.0 | all-reduce | flops 448 | bytes 3584 | tf_op jit(solution)/shard_map/psum | solution.py:101
  213.9 11.8 %all-reduce.1 = (f32[64]{0:T(128)S(1)}, f32[64]{0:T(128)S(1)}) all-reduce(f32[64]{0:T(128)S(1)} %get-tuple-element.3, f32[64]{0:T(128)S(1)} %get-tuple-element.2), channel_id=1, replica_groups=mesh['samp'=8,'cpg'=4] {'samp'}, use_global_device_ids=true, to_apply=%region_58.0 | all-reduce | flops 128 | bytes 1024 | tf_op jit(solution)/shard_map/psum | solution.py:104
  225.7 3.6 %collective-permute-start = (f32[8]{0:T(128)S(1)}, f32[8]{0:T(128)S(1)}, u32[]{:S(2)}, u32[]{:S(2)}) collective-permute-start(f32[8]{0:T(128)S(1)} %get-tuple-element.81), channel_id=1, source_target_pairs={{0,1},{1,2},{2,3},{4,5},{5,6},{6,7},{8,9},{9,10},{10,11},{12,13},{... | collective-permute-start | bytes 104 | tf_op jit(solution)/shard_map/ppermute | solution.py:21
  229.4 1.3 collective-permute-start.1
  230.7 4.2 %collective-permute-done.1 = f32[8]{0:T(128)S(1)} collective-permute-done((f32[8]{0:T(128)S(1)}, f32[8]{0:T(128)S(1)}, u32[]{:S(2)}, u32[]{:S(2)}) %collective-permute-start.1) | collective-permute-done | bytes 64 | tf_op jit(solution)/shard_map/ppermute | solution.py:22
  235.0 0.6 add_divide_fusion.4
  (25 shorter events, 1.9 us)
Async XLA Ops:
  7.2 33.2 %all-gather.3.cloned.1.call-start = ((), (), s32[]{:S(2)}) async-start(), calls=%async_computation.1 | async-start | bytes 2359296 | tf_op jit(solution)/shard_map/all_gather | solution.py:92
  9.3 60.8 %all-gather.5.cloned.1.call-start = ((), (), s32[]{:S(2)}) async-start(), calls=%async_computation.2 | async-start | bytes 2359296 | tf_op jit(solution)/shard_map/all_gather | solution.py:93
  10.0 148.1 %reduce-scatter.2.cloned.1.call-start = ((), (), s32[]{:S(2)}) async-start(), calls=%async_computation.3 | async-start | bytes 5242880 | tf_op jit(solution)/shard_map/reduce_scatter | solution.py:106
  81.1 0.7 copy-start.2
  81.1 0.8 copy-start.1
  158.1 30.1 %copy-start = (f32[64,4096]{1,0:T(8,128)S(1)}, f32[64,4096]{1,0:T(8,128)}, u32[]{:S(2)}) copy-start(f32[64,4096]{1,0:T(8,128)} %reduce-scatter.2.cloned.1.call-done) | copy-start | bytes 3145732
  174.4 60.5 %copy-start.3 = (s32[64]{0:T(128)S(1)}, s32[64]{0:T(128)}, u32[]{:S(2)}) copy-start(s32[64]{0:T(128)} %param.13) | copy-start | bytes 772
  225.7 5.0 %collective-permute-start = (f32[8]{0:T(128)S(1)}, f32[8]{0:T(128)S(1)}, u32[]{:S(2)}, u32[]{:S(2)}) collective-permute-start(f32[8]{0:T(128)S(1)} %get-tuple-element.81), channel_id=1, source_target_pairs={{0,1},{1,2},{2,3},{4,5},{5,6},{6,7},{8,9},{9,10},{10,11},{12,13},{... | collective-permute-start | bytes 104 | tf_op jit(solution)/shard_map/ppermute | solution.py:21
  229.4 5.5 %collective-permute-start.1 = (f32[8]{0:T(128)S(1)}, f32[8]{0:T(128)S(1)}, u32[]{:S(2)}, u32[]{:S(2)}) collective-permute-start(f32[8]{0:T(128)S(1)} %get-tuple-element.82), channel_id=1, source_target_pairs={{1,0},{2,1},{3,2},{5,4},{6,5},{7,6},{9,8},{10,9},{11,10},{13,12},{... | collective-permute-start | bytes 104 | tf_op jit(solution)/shard_map/ppermute | solution.py:22
Sparse Core Ops, SparseCore 0:
  9.9 30.4 all-gather.2
  42.3 27.7 all-gather.4
  81.3 76.7 reduce-scatter.1
where the time goes:
time: 243 us; the launch traced here: 242 us
  waiting for transfers between devices  132 us (54%)
  blocking collectives  60.5 us (25%)
  matrix products  17.4 us (7%)
  between operations  13.8 us (6%)
  other arithmetic  11.4 us (5%)
  starting transfers between devices  5.05 us (2%)
    reduce_scatter x1, waiting for transfers between devices, shards(): lax.psum_scatter(jnp.concatenate([jnp.dot(all_resp, eigvecs, preferred_el...  75.6 us
    psum x4, blocking collectives, fit_block(): return lax.psum(partials, 'samp')  48.7 us
    all_gather x1, waiting for transfers between devices, shards(): lax.all_gather(weighted, 'samp', axis=0, tiled=True)  30.3 us
    all_gather x1, waiting for transfers between devices, shards(): lax.all_gather(design, 'samp', axis=0, tiled=True)  21 us
    psum x1, blocking collectives, score_block(): return lax.psum(partials, 'samp')  11.8 us
    dot_general x1, matrix products, shards(): jnp.dot(all_design, eigvecs, preferred_element_type=jnp.float32)  8.71 us
    dot_general x1, matrix products, shards(): jnp.dot(all_resp, eigvecs, preferred_element_type=jnp.float32)  8.71 us
  transfers between devices with their start and end apart: 5, of which 4 were waited for; matrix products, arithmetic and copies ran while one was open for 4% of the time, Pallas kernels for 0%

commit v1 on v0

v1 whole, which is shorter than its diff:
```python
import functools

import jax
import jax.numpy as jnp
from jax import lax
from jax.experimental import pallas as pl
from jax.experimental.pallas import tpu as pltpu
from jax.sharding import PartitionSpec as P

ITERS = 4
HALO = 8
EPSILON = 1e-06
band_width = 1000.0
MESH = pl.DeviceIdType.MESH
LANES = 128


def fit_kernel(n, cpgs, a_ref, b_ref, lam_ref, band_ref, out_ref, p_ref, q_ref, r_ref, l_ref, send, recv, edge, zsend, ssem, rsem, esem, fsem):
    me = lax.axis_index("samp")
    mz = lax.axis_index("cpg")
    block = a_ref.shape[0]
    fold = LANES // block
    rows = a_ref.shape[1] // fold
    edge[...] = jnp.zeros_like(edge)

    barrier = pltpu.get_barrier_semaphore()
    for j in range(1, n):
        pl.semaphore_signal(barrier, inc=1, device_id={"samp": lax.rem(me + j, n)}, device_id_type=MESH)

    for other in (lax.rem(mz + 1, cpgs), lax.rem(mz + cpgs - 1, cpgs)):
        pl.semaphore_signal(barrier, inc=1, device_id={"cpg": other}, device_id_type=MESH)

    def folded(ref):
        parts = [ref[:, pl.ds(g * rows, rows)].astype(jnp.float32) for g in range(fold)]
        return jnp.concatenate(parts, axis=0).T

    a = folded(a_ref)
    b = folded(b_ref)
    p_ref[...] = a * b
    q_ref[...] = b * b
    r_ref[...] = a * a
    lam_parts = [jnp.broadcast_to(lam_ref[:, pl.ds(g * rows, rows)], (block, rows)) for g in range(fold)]
    l_ref[...] = jnp.concatenate(lam_parts, axis=0).T

    pl.semaphore_wait(barrier, n + 1)

    step = 64

    def sums(log_scale, full):
        scale = jnp.exp(log_scale)

        def body(i, acc):
            at = pl.ds(pl.multiple_of(i * step, step), step)
            lam = l_ref[at, :]
            inv = 1.0 / (scale * lam + 1.0)
            p = p_ref[at, :]
            q = q_ref[at, :]
            terms = [p * inv, q * inv]
            if full:
                lev = lam * inv
                s = lev * inv
                terms += [lev, lev * lev, s * r_ref[at, :], s * p, s * q]
            terms = [t.reshape(step // 8, 8, LANES).sum(axis=0) for t in terms]
            return tuple(x + y for x, y in zip(acc, terms))

        count = 7 if full else 2
        acc = lax.fori_loop(0, rows // step, body, tuple(jnp.zeros((8, LANES), jnp.float32) for _ in range(count)))
        flat = []
        for x in acc:
            row = jnp.sum(x, axis=0, keepdims=True)
            total = row
            for g in range(1, fold):
                total = total + pltpu.roll(row, g * block, 1)
            flat.append(total)
        flat += [jnp.zeros((1, LANES), jnp.float32)] * (8 - count)
        return jnp.concatenate(flat, axis=0)

    def total(it, value):
        send[it] = value
        copies = []
        for j in range(1, n):
            copies.append(pltpu.make_async_remote_copy(
                src_ref=send.at[it], dst_ref=recv.at[it, j],
                send_sem=ssem.at[it, j], recv_sem=rsem.at[it, j],
                device_id={"samp": lax.rem(me + j, n)}, device_id_type=MESH))
        for c in copies:
            c.start()
        recv[it, 0] = value
        for c in copies:
            c.wait_recv()
        out = jnp.zeros((8, LANES), jnp.float32)
        for d in range(n):
            out = out + recv[it, lax.rem(me - d + n, n)]
        for c in copies:
            c.wait_send()
        return out

    log_scale = jnp.zeros((1, LANES), jnp.float32)
    for it in range(ITERS):
        t = total(it, sums(log_scale, True))
        crossed, energy, traced, fisher = t[0:1], t[1:2] + EPSILON, t[2:3], t[3:4]
        effect = crossed / energy
        spread = t[4:5] - 2.0 * effect * t[5:6] + effect * effect * t[6:7]
        gradient = 0.5 * (spread - traced)
        log_scale = log_scale + jnp.tanh(gradient / (jnp.exp(log_scale) * (0.5 * fisher)))
    t = total(ITERS, sums(log_scale, False))
    z = t[0:1] / jnp.sqrt(t[1:2] + EPSILON)
    z = jnp.broadcast_to(z, (8, LANES))
    zsend[...] = z
    down = pltpu.make_async_remote_copy(
        src_ref=zsend, dst_ref=edge.at[1], send_sem=esem.at[0], recv_sem=fsem.at[1],
        device_id={"cpg": lax.max(mz - 1, 0)}, device_id_type=MESH)
    up = pltpu.make_async_remote_copy(
        src_ref=zsend, dst_ref=edge.at[0], send_sem=esem.at[1], recv_sem=fsem.at[0],
        device_id={"cpg": lax.min(mz + 1, cpgs - 1)}, device_id_type=MESH)

    @pl.when(mz > 0)
    def _():
        down.start()

    @pl.when(mz < cpgs - 1)
    def _():
        up.start()

    @pl.when(mz > 0)
    def _():
        down.wait_send()
        up.wait_recv()

    @pl.when(mz < cpgs - 1)
    def _():
        up.wait_send()
        down.wait_recv()

    lane = lax.broadcasted_iota(jnp.int32, (8, LANES), 1)
    wide = jnp.where(lane < block, z, jnp.where(lane < block + HALO, edge[1], edge[0]))
    acc = jnp.zeros((8, LANES), jnp.float32)
    norm = jnp.zeros((8, LANES), jnp.float32)
    for o in range(2 * HALO + 1):
        shift = (HALO - o) % LANES
        near = pltpu.roll(wide, shift, 1) if shift else wide
        c = band_ref[o : o + 1, :]
        acc = acc + c * near
        norm = norm + c
    row = lax.broadcasted_iota(jnp.int32, (8, LANES), 0)
    out_ref[...] = jnp.where(row == 0, acc / norm, jnp.broadcast_to(log_scale, (8, LANES)))


def fit(a, b, lam, band, n, cpgs):
    block, comps = a.shape
    fold = LANES // block
    rows = comps // fold
    big = pltpu.VMEM((rows, LANES), jnp.float32)
    return pl.pallas_call(
        functools.partial(fit_kernel, n, cpgs),
        out_shape=jax.ShapeDtypeStruct((8, LANES), jnp.float32),
        in_specs=[pl.BlockSpec(memory_space=pltpu.VMEM)] * 4,
        out_specs=pl.BlockSpec(memory_space=pltpu.VMEM),
        scratch_shapes=[
            big, big, big, big,
            pltpu.VMEM((ITERS + 1, 8, LANES), jnp.float32),
            pltpu.VMEM((ITERS + 1, n, 8, LANES), jnp.float32),
            pltpu.VMEM((2, 8, LANES), jnp.float32),
            pltpu.VMEM((8, LANES), jnp.float32),
            pltpu.SemaphoreType.DMA((ITERS + 1, n)),
            pltpu.SemaphoreType.DMA((ITERS + 1, n)),
            pltpu.SemaphoreType.DMA((2,)),
            pltpu.SemaphoreType.DMA((2,)),
        ],
        compiler_params=pltpu.CompilerParams(collective_id=1, has_side_effects=True),
        cost_estimate=pl.CostEstimate(flops=20_000_000, bytes_accessed=2_000_000, transcendentals=0),
        name="fit",
    )(a, b, lam, band)


CHUNK = 256


def rotate_kernel(n, cpgs, w_ref, d_ref, v_hbm, a_ref, b_ref, g, v, part, sent, below, above, vsem, gs, gr, ss, bs, us):
    me = lax.axis_index("samp")
    mz = lax.axis_index("cpg")
    each = w_ref.shape[0]
    total = each * n
    block = total // cpgs
    chunks = v.shape[0]
    bits = [1 << i for i in range(1, n.bit_length() - 1)]
    orders = (bits, bits[::-1])
    inputs = (w_ref, d_ref)

    def load(c):
        return pltpu.make_async_copy(v_hbm.at[:, pl.ds(pl.multiple_of(c * CHUNK, CHUNK), CHUNK)], v.at[c], vsem.at[c])

    for c in range(chunks):
        load(c).start()

    def flipped(mask):
        out = me
        bit = 1
        while bit <= mask:
            if mask & bit:
                out = out + bit - 2 * bit * lax.rem(lax.div(me, bit), 2)
            bit *= 2
        return out

    barrier = pltpu.get_barrier_semaphore()
    for bit in [1] + bits:
        pl.semaphore_signal(barrier, inc=1, device_id={"samp": flipped(bit)}, device_id_type=MESH)
    for other in (lax.rem(mz + 1, cpgs), lax.rem(mz + cpgs - 1, cpgs)):
        pl.semaphore_signal(barrier, inc=1, device_id={"cpg": other}, device_id_type=MESH)
    for k in range(2):
        g[pl.ds(pl.multiple_of(k * total + me * each, each), each), :] = inputs[k][...]
    pl.semaphore_wait(barrier, len(bits) + 3)

    def rows(k, mask):
        return pl.ds(pl.multiple_of(k * total + flipped(mask) * each, each), each)

    def hop(k, mask, bit):
        src = g.at[rows(k, mask)] if mask else inputs[k]
        return pltpu.make_async_remote_copy(
            src_ref=src, dst_ref=g.at[rows(k, mask)], send_sem=gs.at[k, mask | bit], recv_sem=gr.at[k, mask | bit],
            device_id={"samp": flipped(bit)}, device_id_type=MESH)

    started = []

    def send(k, mask, bit):
        copy = hop(k, mask, bit)
        copy.start()
        started.append(copy)

    def arrive(k, mask):
        pltpu.make_async_remote_copy(
            src_ref=inputs[k], dst_ref=g.at[rows(k, mask)], send_sem=gs.at[k, mask], recv_sem=gr.at[k, mask],
            device_id={"samp": flipped(1)}, device_id_type=MESH).wait_recv()

    for s in range(len(bits)):
        for k in range(2):
            send(k, 0, orders[k][s])
    for k in range(2):
        send(k, 0, 1)
    held = [[0], [0]]
    for s in range(len(bits)):
        for k in range(2):
            new = [m | orders[k][s] for m in held[k]]
            for m in new:
                arrive(k, m)
                for bit in orders[k][s + 1 :]:
                    send(k, m, bit)
                send(k, m, 1)
            held[k] += new
    for k in range(2):
        for m in held[k]:
            arrive(k, m | 1)

    def hop_up(c, d):
        return pltpu.make_async_remote_copy(
            src_ref=sent.at[c, d], dst_ref=below.at[c, d], send_sem=ss.at[c, d], recv_sem=bs.at[c, d],
            device_id={"cpg": lax.min(mz + 1, cpgs - 1)}, device_id_type=MESH)

    def hop_down(c, d):
        return pltpu.make_async_remote_copy(
            src_ref=sent.at[c, d], dst_ref=above.at[c, d], send_sem=ss.at[c, d], recv_sem=us.at[c, d],
            device_id={"cpg": lax.max(mz - 1, 0)}, device_id_type=MESH)

    def own(c, d, k):
        return part[c, pl.ds(pl.multiple_of(k * total + d * block, block), block), :]

    def pass_on(c, d, hop_of, landed, first):
        @pl.when(first)
        def _():
            for k in range(2):
                sent[c, d, pl.ds(k * block, block), :] = own(c, d, k).astype(jnp.bfloat16)

        @pl.when(jnp.logical_not(first))
        def _():
            hop_of(c, d).wait_recv()
            for k in range(2):
                at = pl.ds(k * block, block)
                sent[c, d, at, :] = (own(c, d, k) + landed[c, d, at, :].astype(jnp.float32)).astype(jnp.bfloat16)

        hop_of(c, d).start()

    def turn(t, carry):
        @pl.when(t < chunks)
        def _():
            load(t).wait()
            part[t] = jnp.dot(g[...], v[t], preferred_element_type=jnp.float32)

        cu = t - mz

        @pl.when((cu >= 0) & (cu < chunks))
        def _():
            def body(i, carry):
                pass_on(cu, cpgs - 1 - i, hop_up, below, mz == 0)
                return carry

            lax.fori_loop(0, cpgs - 1 - mz, body, 0)

        cd = t - (cpgs - 1 - mz)

        @pl.when((cd >= 0) & (cd < chunks))
        def _():
            def body(i, carry):
                pass_on(cd, i, hop_down, above, mz == cpgs - 1)
                return carry

            lax.fori_loop(0, mz, body, 0)

        return carry

    lax.fori_loop(0, chunks + cpgs - 1, turn, 0)

    def finish(c, carry):
        cols = pl.ds(pl.multiple_of(c * CHUNK, CHUNK), CHUNK)
        outs = (a_ref, b_ref)
        for k in range(2):
            outs[k][:, cols] = own(c, mz, k)

        @pl.when(mz > 0)
        def _():
            hop_up(c, mz).wait_recv()
            for k in range(2):
                outs[k][:, cols] += below[c, mz, pl.ds(k * block, block), :].astype(jnp.float32)

        @pl.when(mz < cpgs - 1)
        def _():
            hop_down(c, mz).wait_recv()
            for k in range(2):
                outs[k][:, cols] += above[c, mz, pl.ds(k * block, block), :].astype(jnp.float32)

        return carry

    lax.fori_loop(0, chunks, finish, 0)

    def drain(c, carry):
        for d in range(cpgs):
            @pl.when(d != mz)
            def _():
                hop_up(c, d).wait_send()
        return carry

    lax.fori_loop(0, chunks, drain, 0)
    for copy in started:
        copy.wait_send()


def rotate(weighted, design, eigvecs, n, cpgs):
    each, samples = weighted.shape
    comps = eigvecs.shape[1]
    total = each * n
    block = total // cpgs
    chunks = comps // CHUNK
    travel = pltpu.VMEM((chunks, cpgs, 2 * block, CHUNK), jnp.bfloat16)
    piece = pltpu.SemaphoreType.DMA((chunks, cpgs))
    out = jax.ShapeDtypeStruct((block, comps), jnp.float32)
    vmem = pl.BlockSpec(memory_space=pltpu.VMEM)
    return pl.pallas_call(
        functools.partial(rotate_kernel, n, cpgs),
        out_shape=(out, out),
        in_specs=[vmem, vmem, pl.BlockSpec(memory_space=pl.ANY)],
        out_specs=(vmem, vmem),
        scratch_shapes=[
            pltpu.VMEM((2 * total, samples), jnp.bfloat16),
            pltpu.VMEM((chunks, samples, CHUNK), jnp.bfloat16),
            pltpu.VMEM((chunks, 2 * total, CHUNK), jnp.float32),
            travel, travel, travel,
            pltpu.SemaphoreType.DMA((chunks,)),
            pltpu.SemaphoreType.DMA((2, n)),
            pltpu.SemaphoreType.DMA((2, n)),
            piece, piece, piece,
        ],
        compiler_params=pltpu.CompilerParams(collective_id=2, has_side_effects=True, vmem_limit_bytes=60 * 1024 * 1024),
        cost_estimate=pl.CostEstimate(flops=4 * total * samples * comps, bytes_accessed=2 * samples * comps, transcendentals=0),
        name="rotate",
    )(weighted, design, eigvecs)


def band_of(positions, reaches):
    block = reaches.shape[0]
    total = block * lax.axis_size("cpg")
    base = lax.axis_index("cpg") * block
    places = lax.dynamic_slice_in_dim(jnp.pad(positions.astype(jnp.float32), HALO), base, block + 2 * HALO, 0)
    centre = places[HALO : HALO + block]
    index = jnp.arange(2 * HALO + 1, dtype=jnp.int32)[:, None] + jnp.arange(block, dtype=jnp.int32)[None, :]
    near = jnp.stack([places[o : o + block] for o in range(2 * HALO + 1)])
    at = index + base - HALO
    offset = jnp.abs(jnp.arange(2 * HALO + 1, dtype=jnp.int32) - HALO)[:, None]
    keep = (at >= 0) & (at < total) & (offset <= reaches[None, :])
    band = jnp.where(keep, jnp.exp(-jnp.abs(near - centre[None, :]) / band_width), 0.0)
    return jnp.pad(band, ((0, 7), (0, LANES - block)), constant_values=0.0)


def shards(responses, weights, phenotype, eigvecs, eigvals, positions, reaches):
    root_weight = jnp.sqrt(weights.astype(jnp.float32))
    weighted = (root_weight * responses.astype(jnp.float32)).astype(jnp.bfloat16)
    design = (root_weight * phenotype[None, :]).astype(jnp.bfloat16)

    n, cpgs = lax.axis_size("samp"), lax.axis_size("cpg")
    rot_resp, rot_design = rotate(weighted, design, eigvecs, n, cpgs)
    out = fit(rot_resp, rot_design, eigvals[None, :], band_of(positions, reaches), n, cpgs)
    block = reaches.shape[0]
    return (out[0, :block], out[1, :block])


def solution(mesh):
    in_specs = (P("samp", "cpg"), P("samp", "cpg"), P("cpg"), P("cpg", "samp"), P("samp"), P(), P("cpg"))
    out_specs = (P("cpg"), P("cpg"))
    return jax.shard_map(shards, mesh=mesh, in_specs=in_specs, out_specs=out_specs, check_vma=False)
```

time: 243 us -> 98.9 us (0.41)
  waiting for transfers between devices: 132 us -> 0 us
  Pallas kernels: 0 us -> 93.7 us
  blocking collectives: 60.5 us -> 0 us
  matrix products: 17.4 us -> 0 us
  between operations: 13.8 us -> 0.7 us
  other arithmetic: 11.4 us -> 2.15 us
  starting transfers between devices: 5.05 us -> 0 us
    pallas_call x0 -> x2, Pallas kernels: none -> 93.7 us  [the longest x1 68.2 us: rotate(): pl.pallas_call(functools.partial(rotate_kernel, n, cpgs), out_shape=(out,...]
    reduce_scatter x1 -> x0, waiting for transfers between devices: 75.6 us -> none  [shards(): lax.psum_scatter(jnp.concatenate([jnp.dot(all_resp, eigvecs, preferred_el...]
    psum x5 -> x0, blocking collectives: 60.5 us -> none  [the longest x4 48.7 us: fit_block(): return lax.psum(partials, 'samp')]
    all_gather x2 -> x0, waiting for transfers between devices: 51.3 us -> none  [the longest x1 30.3 us: shards(): lax.all_gather(weighted, 'samp', axis=0, tiled=True)]
    dot_general x2 -> x0, matrix products: 17.4 us -> none  [the longest x1 8.71 us: shards(): jnp.dot(all_design, eigvecs, preferred_element_type=jnp.float32)]
    reduce_sum x5 -> x0, other arithmetic: 5.12 us -> none  [the longest x4 4.81 us: fit_scores(): energy_part = jnp.sum(design_over * rot_design, axis=sum_axis)]
    ppermute x2 -> x0, starting transfers between devices: 4.93 us -> none  [the longest x1 3.64 us: padded(): before = lax.ppermute(last, axis, up)]
    ppermute x2 -> x0, waiting for transfers between devices: 4.19 us -> none  [the longest x1 4.19 us: padded(): after = lax.ppermute(leading, axis, down)]
  transfers between devices with their start and end apart: 5 -> 0, of which waited for: 4 -> 0; matrix products, arithmetic and copies ran while one was open for 4% -> 0% of each run, Pallas kernels for 0% -> 0%
where the time goes in v1:
time: 98.9 us; the launch traced here: 98.7 us
  Pallas kernels  93.7 us (95%)
  other arithmetic  2.15 us (2%)
  local copies, waits for them, and re-layouts  2.13 us (2%)
    pallas_call x1, Pallas kernels, rotate(): pl.pallas_call(functools.partial(rotate_kernel, n, cpgs), out_shape=(out,...  68.2 us
    pallas_call x1, Pallas kernels, fit(): pl.pallas_call(functools.partial(fit_kernel, n, cpgs), out_shape=jax.Shap...  25.5 us
    convert_element_type x1, other arithmetic, shards(): design = (root_weight * phenotype[None, :]).astype(jnp.bfloat16)  2.07 us

profile of v1, /device:TPU:0, one launch (start us, length us, event | category | flops | bytes accessed | tf_op | source)
XLA Modules:
  0.0 98.7 jit_solution(10438270682915635485)
XLA Ops:
  0.6 0.0 copy-start
  0.6 0.0 copy-start.1
  0.7 2.1 %multiply_convert_fusion = (bf16[32,4096]{1,0:T(8,128)(2,1)}, bf16[32,4096]{1,0:T(8,128)(2,1)}) fusion(bf16[32,4096]{1,0:T(8,128)(2,1)} %param.8, f32[4096]{0:T(1024)} %param.9, bf16[32,4096]{1,0:T(8,128)(2,1)} %param.7), kind=kLoop, calls=%fused_computation | loop fusion | flops 786432 | bytes 1064960 | tf_op jit(solution)/shard_map/convert_element_type | solution.py:395
  2.7 68.2 %rotate.1 = (f32[64,2048]{1,0:T(8,128)}, f32[64,2048]{1,0:T(8,128)}) custom-call(bf16[32,4096]{1,0:T(8,128)(2,1)} %get-tuple-element.7.w_ref, bf16[32,4096]{1,0:T(8,128)(2,1)} %get-tuple-element.6.d_ref, bf16[4096,2048]{1,0:T(8,128)(2,1)} %v_hbm.1), custom_call_target="tpu_custom_call" | custom-call | flops 8589934592 | bytes 16777216 | tf_op jit(solution)/shard_map/rotate/pallas_call | solution.py:356
  70.9 0.0 copy-done
  70.9 0.1 pad_dynamic-slice_fusion
  71.0 0.1 fusion.4
  71.1 0.1 stack.71
  71.2 0.0 copy-done.1
  71.2 0.1 exponential_select_fusion
  71.3 0.6 pad.9.band_ref
  71.9 25.5 %fit.1 = f32[8,128]{1,0:T(8,128)} custom-call(f32[64,2048]{1,0:T(8,128)} %get-tuple-element.4.a_ref, f32[64,2048]{1,0:T(8,128)} %get-tuple-element.5.b_ref, f32[1,2048]{1,0:T(1,128)} %bitcast.39, f32[24,128]{1,0:T(8,128)} %pad.9.band_ref), custom_call_target="tpu_custom_call" | custom-call | flops 20000000 | bytes 2000000 | tf_op jit(solution)/shard_map/fit/pallas_call | solution.py:154
  97.4 1.3 %slice_bitcast_fusion = (f32[64]{0:T(128)}, f32[64]{0:T(128)}) fusion(f32[8,128]{1,0:T(8,128)} %fit.1), kind=kLoop, calls=%fused_computation.10 | loop fusion | bytes 1024 | tf_op jit(solution)/shard_map/squeeze | solution.py:401
  (2 shorter events, 0.0 us)
Async XLA Ops:
  0.6 70.3 %copy-start = (s32[256]{0:T(256)S(1)}, s32[256]{0:T(256)}, u32[]{:S(2)}) copy-start(s32[256]{0:T(256)} %param.12) | copy-start | bytes 3076
  0.6 70.5 %copy-start.1 = (s32[64]{0:T(128)S(1)}, s32[64]{0:T(128)}, u32[]{:S(2)}) copy-start(s32[64]{0:T(128)} %param.13) | copy-start | bytes 772

commit v2 on v1

--- a/solution.py
+++ b/solution.py
@@ -183,8 +183,10 @@
     total = each * n
     block = total // cpgs
     chunks = v.shape[0]
+    units = 2 * chunks
     bits = [1 << i for i in range(1, n.bit_length() - 1)]
     orders = (bits, bits[::-1])
+    half = w_ref.shape[1] // 2
     inputs = (w_ref, d_ref)
 
     def load(c):
@@ -214,42 +216,57 @@
     def rows(k, mask):
         return pl.ds(pl.multiple_of(k * total + flipped(mask) * each, each), each)
 
-    def hop(k, mask, bit):
-        src = g.at[rows(k, mask)] if mask else inputs[k]
+    def hop(k, h, mask, bit):
+        cols = pl.ds(h * half, half)
+        dst = g.at[rows(k, mask), cols]
         return pltpu.make_async_remote_copy(
-            src_ref=src, dst_ref=g.at[rows(k, mask)], send_sem=gs.at[k, mask | bit], recv_sem=gr.at[k, mask | bit],
+            src_ref=dst if mask else inputs[k].at[:, cols], dst_ref=dst,
+            send_sem=gs.at[k, h, mask | bit], recv_sem=gr.at[k, h, mask | bit],
             device_id={"samp": flipped(bit)}, device_id_type=MESH)
 
     started = []
 
-    def send(k, mask, bit):
-        copy = hop(k, mask, bit)
-        copy.start()
-        started.append(copy)
-
-    def arrive(k, mask):
+    def send(k, h, mask, bit):
+        hop(k, h, mask, bit).start()
+        started.append((k, h, mask, bit))
+
+    def arrive(k, h, mask):
+        cols = pl.ds(h * half, half)
         pltpu.make_async_remote_copy(
-            src_ref=inputs[k], dst_ref=g.at[rows(k, mask)], send_sem=gs.at[k, mask], recv_sem=gr.at[k, mask],
+            src_ref=inputs[k].at[:, cols], dst_ref=g.at[rows(k, mask), cols],
+            send_sem=gs.at[k, h, mask], recv_sem=gr.at[k, h, mask],
             device_id={"samp": flipped(1)}, device_id_type=MESH).wait_recv()
 
-    for s in range(len(bits)):
-        for k in range(2):
-            send(k, 0, orders[k][s])
-    for k in range(2):
-        send(k, 0, 1)
-    held = [[0], [0]]
-    for s in range(len(bits)):
-        for k in range(2):
-            new = [m | orders[k][s] for m in held[k]]
+    def begin(k):
+        for s in range(len(bits)):
+            for h in range(2):
+                send(k, h, 0, orders[h][s])
+        for h in range(2):
+            send(k, h, 0, 1)
+
+    held = [[[0], [0]], [[0], [0]]]
+
+    def relay(k, s):
+        for h in range(2):
+            new = [m | orders[h][s] for m in held[k][h]]
             for m in new:
-                arrive(k, m)
-                for bit in orders[k][s + 1 :]:
-                    send(k, m, bit)
-                send(k, m, 1)
-            held[k] += new
-    for k in range(2):
-        for m in held[k]:
-            arrive(k, m | 1)
+                arrive(k, h, m)
+                for bit in orders[h][s + 1 :]:
+                    send(k, h, m, bit)
+                send(k, h, m, 1)
+            held[k][h] += new
+
+    def complete(k):
+        for h in range(2):
+            for m in held[k][h]:
+                arrive(k, h, m | 1)
+
+    begin(0)
+    for s in range(len(bits) - 1):
+        relay(0, s)
+    begin(1)
+    relay(0, len(bits) - 1)
+    complete(0)
 
     def hop_up(c, d):
         return pltpu.make_async_remote_copy(
@@ -261,33 +278,45 @@
             src_ref=sent.at[c, d], dst_ref=above.at[c, d], send_sem=ss.at[c, d], recv_sem=us.at[c, d],
             device_id={"cpg": lax.max(mz - 1, 0)}, device_id_type=MESH)
 
-    def own(c, d, k):
-        return part[c, pl.ds(pl.multiple_of(k * total + d * block, block), block), :]
+    def own(u, d):
+        return part[u, pl.ds(pl.multiple_of(d * block, block), block), :]
 
     def pass_on(c, d, hop_of, landed, first):
         @pl.when(first)
         def _():
-            for k in range(2):
-                sent[c, d, pl.ds(k * block, block), :] = own(c, d, k).astype(jnp.bfloat16)
+            sent[c, d] = own(c, d).astype(jnp.bfloat16)
 
         @pl.when(jnp.logical_not(first))
         def _():
             hop_of(c, d).wait_recv()
-            for k in range(2):
-                at = pl.ds(k * block, block)
-                sent[c, d, at, :] = (own(c, d, k) + landed[c, d, at, :].astype(jnp.float32)).astype(jnp.bfloat16)
+            sent[c, d] = (own(c, d) + landed[c, d].astype(jnp.float32)).astype(jnp.bfloat16)
 
         hop_of(c, d).start()
 
     def turn(t, carry):
+        for s in range(len(bits) - 1):
+            @pl.when(t == chunks * (s + 1) // len(bits) - 1)
+            def _():
+                relay(1, s)
+
+        @pl.when(t == chunks)
+        def _():
+            relay(1, len(bits) - 1)
+            complete(1)
+
         @pl.when(t < chunks)
         def _():
             load(t).wait()
-            part[t] = jnp.dot(g[...], v[t], preferred_element_type=jnp.float32)
+
+        @pl.when(t < units)
+        def _():
+            k = lax.div(t, chunks)
+            left = g[pl.ds(pl.multiple_of(k * total, total), total), :]
+            part[t] = jnp.dot(left, v[t - k * chunks], preferred_element_type=jnp.float32)
 
         cu = t - mz
 
-        @pl.when((cu >= 0) & (cu < chunks))
+        @pl.when((cu >= 0) & (cu < units))
         def _():
             def body(i, carry):
                 pass_on(cu, cpgs - 1 - i, hop_up, below, mz == 0)
@@ -297,7 +326,7 @@
 
         cd = t - (cpgs - 1 - mz)
 
-        @pl.when((cd >= 0) & (cd < chunks))
+        @pl.when((cd >= 0) & (cd < units))
         def _():
             def body(i, carry):
                 pass_on(cd, i, hop_down, above, mz == cpgs - 1)
@@ -307,25 +336,23 @@
 
         return carry
 
-    lax.fori_loop(0, chunks + cpgs - 1, turn, 0)
+    lax.fori_loop(0, units + cpgs - 1, turn, 0)
 
     def finish(c, carry):
         cols = pl.ds(pl.multiple_of(c * CHUNK, CHUNK), CHUNK)
-        outs = (a_ref, b_ref)
-        for k in range(2):
-            outs[k][:, cols] = own(c, mz, k)
-
-        @pl.when(mz > 0)
-        def _():
-            hop_up(c, mz).wait_recv()
-            for k in range(2):
-                outs[k][:, cols] += below[c, mz, pl.ds(k * block, block), :].astype(jnp.float32)
-
-        @pl.when(mz < cpgs - 1)
-        def _():
-            hop_down(c, mz).wait_recv()
-            for k in range(2):
-                outs[k][:, cols] += above[c, mz, pl.ds(k * block, block), :].astype(jnp.float32)
+        for k, out in enumerate((a_ref, b_ref)):
+            u = k * chunks + c
+            out[:, cols] = own(u, mz)
+
+            @pl.when(mz > 0)
+            def _():
+                hop_up(u, mz).wait_recv()
+                out[:, cols] += below[u, mz].astype(jnp.float32)
+
+            @pl.when(mz < cpgs - 1)
+            def _():
+                hop_down(u, mz).wait_recv()
+                out[:, cols] += above[u, mz].astype(jnp.float32)
 
         return carry
 
@@ -338,9 +365,9 @@
                 hop_up(c, d).wait_send()
         return carry
 
-    lax.fori_loop(0, chunks, drain, 0)
-    for copy in started:
-        copy.wait_send()
+    lax.fori_loop(0, units, drain, 0)
+    for item in started:
+        hop(*item).wait_send()
 
 
 def rotate(weighted, design, eigvecs, n, cpgs):
@@ -349,8 +376,8 @@
     total = each * n
     block = total // cpgs
     chunks = comps // CHUNK
-    travel = pltpu.VMEM((chunks, cpgs, 2 * block, CHUNK), jnp.bfloat16)
-    piece = pltpu.SemaphoreType.DMA((chunks, cpgs))
+    travel = pltpu.VMEM((2 * chunks, cpgs, block, CHUNK), jnp.bfloat16)
+    piece = pltpu.SemaphoreType.DMA((2 * chunks, cpgs))
     out = jax.ShapeDtypeStruct((block, comps), jnp.float32)
     vmem = pl.BlockSpec(memory_space=pltpu.VMEM)
     return pl.pallas_call(
@@ -361,11 +388,11 @@
         scratch_shapes=[
             pltpu.VMEM((2 * total, samples), jnp.bfloat16),
             pltpu.VMEM((chunks, samples, CHUNK), jnp.bfloat16),
-            pltpu.VMEM((chunks, 2 * total, CHUNK), jnp.float32),
+            pltpu.VMEM((2 * chunks, total, CHUNK), jnp.float32),
             travel, travel, travel,
             pltpu.SemaphoreType.DMA((chunks,)),
-            pltpu.SemaphoreType.DMA((2, n)),
-            pltpu.SemaphoreType.DMA((2, n)),
+            pltpu.SemaphoreType.DMA((2, 2, n)),
+            pltpu.SemaphoreType.DMA((2, 2, n)),
             piece, piece, piece,
         ],
         compiler_params=pltpu.CompilerParams(collective_id=2, has_side_effects=True, vmem_limit_bytes=60 * 1024 * 1024),

time: 98.9 us -> 95.9 us (0.970)
  Pallas kernels: 93.7 us -> 90.7 us
    pallas_call x1, Pallas kernels: 68.2 us -> 66.2 us  [rotate(): pl.pallas_call(functools.partial(rotate_kernel, n, cpgs), out_shape=(out,...]
where the time goes in v2:
time: 95.9 us; the launch traced here: 95.7 us
  Pallas kernels  90.7 us (95%)
  other arithmetic  2.15 us (2%)
  local copies, waits for them, and re-layouts  2.13 us (2%)
    pallas_call x1, Pallas kernels, rotate(): pl.pallas_call(functools.partial(rotate_kernel, n, cpgs), out_shape=(out,...  66.2 us
    pallas_call x1, Pallas kernels, fit(): pl.pallas_call(functools.partial(fit_kernel, n, cpgs), out_shape=jax.Shap...  24.6 us
    convert_element_type x1, other arithmetic, shards(): design = (root_weight * phenotype[None, :]).astype(jnp.bfloat16)  2.07 us

profile of v2, /device:TPU:0, one launch (start us, length us, event | category | flops | bytes accessed | tf_op | source)
XLA Modules:
  0.0 95.7 jit_solution(12622374280202107511)
XLA Ops:
  0.6 0.0 copy-start
  0.6 0.0 copy-start.1
  0.7 2.1 %multiply_convert_fusion = (bf16[32,4096]{1,0:T(8,128)(2,1)}, bf16[32,4096]{1,0:T(8,128)(2,1)}) fusion(bf16[32,4096]{1,0:T(8,128)(2,1)} %param.8, f32[4096]{0:T(1024)} %param.9, bf16[32,4096]{1,0:T(8,128)(2,1)} %param.7), kind=kLoop, calls=%fused_computation | loop fusion | flops 786432 | bytes 1064960 | tf_op jit(solution)/shard_map/convert_element_type | solution.py:422
  2.7 66.2 %rotate.1 = (f32[64,2048]{1,0:T(8,128)}, f32[64,2048]{1,0:T(8,128)}) custom-call(bf16[32,4096]{1,0:T(8,128)(2,1)} %get-tuple-element.7.w_ref, bf16[32,4096]{1,0:T(8,128)(2,1)} %get-tuple-element.6.d_ref, bf16[4096,2048]{1,0:T(8,128)(2,1)} %v_hbm.1), custom_call_target="tpu_custom_call" | custom-call | flops 8589934592 | bytes 16777216 | tf_op jit(solution)/shard_map/rotate/pallas_call | solution.py:383
  68.9 0.0 copy-done
  68.9 0.1 pad_dynamic-slice_fusion
  69.0 0.1 fusion.4
  69.1 0.1 stack.71
  69.2 0.0 copy-done.1
  69.2 0.1 exponential_select_fusion
  69.3 0.6 pad.9.band_ref
  69.9 24.6 %fit.1 = f32[8,128]{1,0:T(8,128)} custom-call(f32[64,2048]{1,0:T(8,128)} %get-tuple-element.4.a_ref, f32[64,2048]{1,0:T(8,128)} %get-tuple-element.5.b_ref, f32[1,2048]{1,0:T(1,128)} %bitcast.39, f32[24,128]{1,0:T(8,128)} %pad.9.band_ref), custom_call_target="tpu_custom_call" | custom-call | flops 20000000 | bytes 2000000 | tf_op jit(solution)/shard_map/fit/pallas_call | solution.py:154
  94.4 1.3 %slice_bitcast_fusion = (f32[64]{0:T(128)}, f32[64]{0:T(128)}) fusion(f32[8,128]{1,0:T(8,128)} %fit.1), kind=kLoop, calls=%fused_computation.10 | loop fusion | bytes 1024 | tf_op jit(solution)/shard_map/squeeze | solution.py:428
  (2 shorter events, 0.0 us)
Async XLA Ops:
  0.6 68.3 %copy-start = (s32[256]{0:T(256)S(1)}, s32[256]{0:T(256)}, u32[]{:S(2)}) copy-start(s32[256]{0:T(256)} %param.12) | copy-start | bytes 3076
  0.6 68.5 %copy-start.1 = (s32[64]{0:T(128)S(1)}, s32[64]{0:T(128)}, u32[]{:S(2)}) copy-start(s32[64]{0:T(128)} %param.13) | copy-start | bytes 772
